TPU v7x, 512 devices: a whole 4x4x16 slice. The times are simulated.
512 devices in a mesh: bytes: 16 (over z), ctx: 8 (over x, core), tp: 4 (over y).
Axes of the slice: x: 4, y: 4, z: 16, core: 2. Of those that a mesh axis runs over, the one named last changes fastest.
Arguments:
- byte_values_sequence: int32 [24576], P(('bytes', 'ctx')), may hold values from 0 to 255
- offsets: int32 [24576], P(('bytes', 'ctx')), may hold values from 0 to 168, as said below
- byte_table: bfloat16 [256, 1024], replicated, may hold values from -6 to 6
- byte_query: bfloat16 [1024, 1024], P(None, 'tp'), may hold values from -1 to 1
- byte_key: bfloat16 [1024, 1024], P(None, 'tp'), may hold values from -16 to 16
- byte_value: bfloat16 [1024, 1024], P(None, 'tp'), may hold values from -0.1875 to 0.1875
- latent_query: bfloat16 [1024, 4096], P(None, ('ctx', 'tp')), may hold values from -1 to 1
- latent_key: bfloat16 [1024, 4096], P(None, ('ctx', 'tp')), may hold values from -16 to 16
- latent_value: bfloat16 [1024, 4096], P(None, ('ctx', 'tp')), may hold values from -0.1875 to 0.1875
- decode_weight: bfloat16 [4096, 1024], P(('ctx', 'tp')), may hold values from -1 to 1
Outputs:
- byte_output: bfloat16 [24576, 1024], P(('bytes', 'ctx'), 'tp')
Inputs may be any that keep to these rules, and one draw needn't show every extreme that they name: offsets[i] is 0 where a patch starts and offsets[i - 1] + 1 elsewhere; the first byte of every device's 192 bytes starts a patch; one device's bytes hold 24 to 72 patch starts and the bytes of the devices of one index of bytes hold at most 384; both most values are reached in every draw.
All inputs are finite; a program needn't handle non-finite values.
Results may differ from a plain program's by a relative error of at most 0.017.
Values may be sent and summed in bfloat16 or wider, within the bound.
No kernel may reach another device: no remote copies, remote signals or barrier semaphores. Data moves between devices by JAX's collectives and lax.ppermute only.
A program may use at most 64 MiB of HBM per device.

v0:
```python
import math
import jax
import jax.numpy as jnp
from jax import lax
from jax.sharding import PartitionSpec as P

DB = 1024
HEADS_B = 16
HEAD_L = 128
EPSILON = 1e-06
NEGATIVE = -1e30
FARAWAY = 1 << 30


def from_behind(value, axis, steps):
    count = lax.axis_size(axis)
    first, last = (max(0, -steps), min(count, count - steps))
    return lax.ppermute(value, axis, [(source, source + steps) for source in range(first, last)])


def copy_for_each(array, axis):
    copies = jnp.broadcast_to(array, (lax.axis_size(axis), *array.shape))
    return lax.all_to_all(copies, axis, split_axis=0, concat_axis=0, tiled=True)


def joined_along(tiles, dim):
    tiles = jnp.moveaxis(tiles, 0, dim)
    lengths = tiles.shape
    return tiles.reshape(*lengths[:dim], lengths[dim] * lengths[dim + 1], *lengths[dim + 2 :])


def collect(array, axis, dim):
    tiles = copy_for_each(array, axis)
    return joined_along(tiles, dim)


def sent_together(arrays, axis, dim, along):
    widths = [a.shape[along] for a in arrays]
    both = jnp.concatenate(arrays, axis=along)
    filled = lax.all_gather(both, axis, axis=dim, tiled=True)
    return tuple(jnp.split(filled, [sum(widths[:k]) for k in range(1, len(widths))], axis=along))


def cut_along(array, dim, count):
    before, after = (array.shape[:dim], array.shape[dim + 1 :])
    return jnp.moveaxis(array.reshape(*before, count, -1, *after), dim, 0)


def sent_and_summed(array, axis, dim):
    tiles = cut_along(array, dim, lax.axis_size(axis))
    arrived = lax.all_to_all(tiles, axis, split_axis=0, concat_axis=0, tiled=True)
    return arrived.astype(jnp.float32).sum(axis=0)


def norm_rows(values):
    values = values.astype(jnp.float32)
    return values * lax.rsqrt(jnp.mean(values * values, axis=-1, keepdims=True) + EPSILON)


def project(inputs, weight):
    return jnp.dot(inputs, weight, preferred_element_type=jnp.float32).astype(jnp.bfloat16)


def byte_project(byte_values_sequence, byte_table, weights):
    onehot = (
        byte_values_sequence[:, None] == jnp.arange(byte_table.shape[0], dtype=jnp.int32)[None, :]
    ).astype(jnp.bfloat16)
    embedded = jnp.dot(onehot, byte_table, preferred_element_type=jnp.float32)
    normed = norm_rows(embedded).astype(jnp.bfloat16)
    return tuple((project(normed, weight) for weight in weights))


def per_device(
    byte_values_sequence,
    offsets,
    byte_table,
    byte_query,
    byte_key,
    byte_value,
    latent_query,
    latent_key,
    latent_value,
    decode_weight,
):
    row_count = byte_values_sequence.shape[0]
    channels = byte_query.shape[1]
    heads_here = HEADS_B * channels // DB
    head_feature_width = channels // heads_here
    ctx_count = lax.axis_size("ctx")
    tp_count = lax.axis_size("tp")
    slot_cap = 3 * row_count // 8
    block_index = lax.axis_index(("bytes", "ctx"))
    byte_window_queries, byte_window_keys, values_b = byte_project(
        byte_values_sequence, byte_table, (byte_query, byte_key, byte_value)
    )
    earlier_ids = from_behind(byte_values_sequence, ("bytes", "ctx"), 1)
    keys_e, values_e = byte_project(earlier_ids, byte_table, (byte_key, byte_value))
    keys_w = jnp.concatenate([keys_e, byte_window_keys], axis=0).reshape(
        2 * row_count, heads_here, head_feature_width
    )
    values_w = jnp.concatenate([values_e, values_b], axis=0).reshape(
        2 * row_count, heads_here, head_feature_width
    )
    queries_w = byte_window_queries.reshape(row_count, heads_here, head_feature_width)
    query_pos = jnp.arange(row_count, dtype=jnp.int32)[:, None]
    key_pos = jnp.arange(2 * row_count, dtype=jnp.int32)[None, :]
    allowed_b = (
        (key_pos > query_pos)
        & (key_pos <= query_pos + row_count)
        & ((key_pos >= row_count) | (block_index > 0))
    )
    scores_b = jnp.einsum(
        "qhd,khd->hqk", queries_w, keys_w, preferred_element_type=jnp.float32
    ) / math.sqrt(head_feature_width)
    scores_b = jnp.where(allowed_b[None], scores_b, NEGATIVE)
    highest_b = jnp.max(scores_b, axis=-1, keepdims=True)
    weights_b = jnp.where(allowed_b[None], jnp.exp(scores_b - highest_b), 0.0)
    totals_b = jnp.sum(weights_b, axis=-1)
    blended = jnp.einsum(
        "hqk,khd->qhd", weights_b.astype(jnp.bfloat16), values_w, preferred_element_type=jnp.float32
    )
    encoded = (blended / totals_b.T[:, :, None]).reshape(row_count, channels).astype(jnp.bfloat16)
    starts = (offsets == 0).astype(jnp.int32)
    local_patch = jnp.cumsum(starts) - 1
    members = local_patch[None, :] == jnp.arange(slot_cap, dtype=jnp.int32)[:, None]
    patch_sums = jnp.dot(members.astype(jnp.bfloat16), encoded, preferred_element_type=jnp.float32)
    lengths = jnp.sum(members.astype(jnp.float32), axis=1)
    pooled = (patch_sums / jnp.maximum(lengths, 1.0)[:, None]).astype(jnp.bfloat16)
    gathered, patch_counts = (
        collect(pooled, ("ctx", "tp"), 0),
        collect(local_patch[-1:] + 1, ("ctx", "tp"), 0),
    )
    features = gathered.reshape(ctx_count, tp_count, slot_cap, channels).transpose(0, 2, 1, 3)
    features = features.reshape(ctx_count * slot_cap, tp_count * channels)
    patch_counts = patch_counts.reshape(ctx_count, tp_count)[:, 0]
    slot_ids = jnp.arange(slot_cap, dtype=jnp.int32)
    block_ids = lax.axis_index("bytes") * ctx_count + jnp.arange(ctx_count, dtype=jnp.int32)
    positions = jnp.where(
        slot_ids[None, :] < patch_counts[:, None],
        block_ids[:, None] * slot_cap + slot_ids[None, :],
        FARAWAY,
    ).reshape(-1)
    capacity = ctx_count * row_count // 4
    running = jnp.cumsum((positions < FARAWAY).astype(jnp.int32))
    targets = jnp.arange(capacity, dtype=jnp.int32)
    chosen = jnp.minimum(jnp.searchsorted(running, targets + 1), running.shape[0] - 1)
    features = features[chosen]
    positions = jnp.where(targets < running[-1], positions[chosen], FARAWAY)
    latent_in = norm_rows(features).astype(jnp.bfloat16)
    queries_l = project(latent_in, latent_query)
    keys_l = project(latent_in, latent_key)
    values_l = project(latent_in, latent_value)
    query_rows = queries_l.shape[0]
    heads_latent = queries_l.shape[1] // HEAD_L
    queries_h = queries_l.reshape(query_rows, heads_latent, HEAD_L)
    initial = (
        jnp.full((heads_latent, query_rows), NEGATIVE, jnp.float32),
        jnp.zeros((heads_latent, query_rows), jnp.float32),
        jnp.zeros((query_rows, heads_latent, HEAD_L), jnp.float32),
    )
    running_state = initial
    keys_p, values_p, places_p = (
        *sent_together((keys_l, values_l), "bytes", 0, 1),
        lax.all_gather(positions, "bytes", axis=0, tiled=True),
    )
    span_rows = keys_p.shape[0]

    def attend_block(state, step_index):
        highest, totals, accumulated = state
        keys_s = lax.dynamic_slice_in_dim(keys_p, step_index * query_rows, query_rows, 0).reshape(
            query_rows, heads_latent, HEAD_L
        )
        values_s = lax.dynamic_slice_in_dim(
            values_p, step_index * query_rows, query_rows, 0
        ).reshape(query_rows, heads_latent, HEAD_L)
        places = lax.dynamic_slice_in_dim(places_p, step_index * query_rows, query_rows, 0)
        attention_scores = jnp.einsum(
            "qhd,khd->hqk", queries_h, keys_s, preferred_element_type=jnp.float32
        ) / math.sqrt(HEAD_L)
        allowed = (places[None, :] <= positions[:, None])[None]
        highest_new = jnp.maximum(
            highest, jnp.max(jnp.where(allowed, attention_scores, NEGATIVE), axis=-1)
        )
        factor = jnp.exp(highest - highest_new)
        weights = jnp.where(allowed, jnp.exp(attention_scores - highest_new[:, :, None]), 0.0)
        totals = totals * factor + jnp.sum(weights, axis=-1)
        mixed_in = jnp.einsum(
            "hqk,khd->qhd",
            weights.astype(jnp.bfloat16),
            values_s,
            preferred_element_type=jnp.float32,
        )
        accumulated = accumulated * factor.T[:, :, None] + mixed_in
        return ((highest_new, totals, accumulated), None)

    running_state, _ = lax.scan(
        attend_block, running_state, jnp.arange(span_rows // query_rows, dtype=jnp.int32)
    )
    highest_l, totals_l, accumulated_l = running_state
    latent_out = (
        (accumulated_l / totals_l.T[:, :, None])
        .reshape(query_rows, heads_latent * HEAD_L)
        .astype(jnp.bfloat16)
    )
    shares = sent_and_summed(
        jnp.dot(latent_out, decode_weight, preferred_element_type=jnp.float32).astype(jnp.bfloat16),
        ("ctx", "tp"),
        0,
    )
    summed = collect(shares.astype(jnp.bfloat16), ("ctx", "tp"), 0).astype(shares.dtype)
    before = jnp.sum(
        jnp.where(jnp.arange(ctx_count, dtype=jnp.int32) < lax.axis_index("ctx"), patch_counts, 0)
    )
    mine = lax.dynamic_slice_in_dim(summed, lax.axis_index("tp") * channels, channels, 1)
    decoded_bytes = mine[before + local_patch]
    return (encoded.astype(jnp.float32) + decoded_bytes).astype(jnp.bfloat16)


def solution(mesh):
    return jax.shard_map(
        per_device,
        mesh=mesh,
        in_specs=(
            P(("bytes", "ctx")),
            P(("bytes", "ctx")),
            P(),
            P(None, "tp"),
            P(None, "tp"),
            P(None, "tp"),
            P(None, ("ctx", "tp")),
            P(None, ("ctx", "tp")),
            P(None, ("ctx", "tp")),
            P(("ctx", "tp"), None),
        ),
        out_specs=P(("bytes", "ctx"), "tp"),
        check_vma=False,
    )
```

profile of v0, /device:TPU:1, one launch (start us, length us, event | category | flops | bytes accessed | tf_op | source)
XLA Modules:
  0.0 257.1 jit_solution(15806933889242681807)
XLA Ops:
  6.5 4.6 %collective-permute-start = (s32[192]{0:T(256)}, s32[192]{0:T(256)S(1)}, u32[]{:S(2)}, u32[]{:S(2)}) collective-permute-start(s32[192]{0:T(256)} %param.14), channel_id=1, source_target_pairs={{0,4},{4,8},{8,12},{12,16},{16,20},{20,24},{24,28},{28,32},{32,36}... | collective-permute-start | bytes 2312 | tf_op jit(solution)/shard_map/ppermute | solution.py:18
  14.9 7.3 %all-to-all-start = ((s32[32,1,1]{2,1,0:T(1,128)}), s32[32,1,1]{2,1,0:T(1,128)S(1)}, u32[]{:S(2)}, u32[]{:S(2)}) async-start(s32[32,1,1]{2,1,0:T(1,128)} %broadcast_in_dim.111), calls=%async_computation | async-start | bytes 32768 | tf_op jit(solution)/shard_map/all_to_all | solution.py:23
  26.6 2.6 %all-to-all-done = s32[32,1,1]{2,1,0:T(1,128)S(1)} async-done(((s32[32,1,1]{2,1,0:T(1,128)}), s32[32,1,1]{2,1,0:T(1,128)S(1)}, u32[]{:S(2)}, u32[]{:S(2)}) %all-to-all-start) | async-done | bytes 160 | tf_op jit(solution)/shard_map/all_to_all | solution.py:23
  33.0 1.3 fusion.25
  37.2 4.8 %all-to-all-start.1 = ((bf16[32,72,256]{2,1,0:T(8,128)(2,1)}), bf16[32,72,256]{2,1,0:T(8,128)(2,1)S(1)}, u32[]{:S(2)}, u32[]{:S(2)}) async-start(bf16[32,72,256]{2,1,0:T(8,128)(2,1)} %broadcast_in_dim.118), calls=%async_computation.1 | async-start | bytes 2359296 | tf_op jit(solution)/shard_map/all_to_all | solution.py:23
  42.0 19.8 %while.39 = (s32[]{:T(128)}, u32[384]{0:T(512)S(1)}, u32[384]{0:T(512)S(1)}, s32[576]{0:T(1024)S(1)}, s32[]{:T(128)}, /*index=5*/s32[]{:T(128)}, s32[]{}) while((s32[]{:T(128)}, u32[384]{0:T(512)S(1)}, u32[384]{0:T(512)S(1)}, s32[576]{0:T(1024)S(1)}, s32[]{:T(128)}, /*index=5*/s32[]{:T(128)}, s32[]{}) %tuple.72), condition=%wide.region_10.11_spmd.clone, body=%wide.region_9.10_spmd.clone.sunk | while | flops 8324 | bytes 29541 | solution.py:146
  42.1 1.9 gather_fusion
  44.1 1.9 gather_fusion
  46.0 1.9 gather_fusion
  48.0 1.9 gather_fusion
  50.0 1.9 gather_fusion
  52.0 1.9 gather_fusion
  54.0 1.9 gather_fusion
  56.0 1.9 gather_fusion
  57.9 1.9 gather_fusion
  59.9 1.9 gather_fusion
  62.7 2.1 gather_fusion.2
  66.9 1.9 gather_fusion.1
  70.1 29.0 %all-gather = s32[16,1,384]{2,1,0:T(1,128)S(1)} all-gather(s32[1,1,384]{2,1,0:T(1,128)S(1)} %reshape.249), channel_id=1, replica_groups=mesh['bytes'=16,'ctx'=8,'tp'=4] {'bytes'}, dimensions={0}, use_global_device_ids=true | all-gather | bytes 26112 | tf_op jit(solution)/shard_map/all_gather | solution.py:164
  99.5 38.2 %all-gather.3.cloned.1.call-done = bf16[6144,256]{0,1:T(8,128)(2,1)} async-done(((bf16[384,256]{0,1:T(8,128)(2,1)}), bf16[6144,256]{0,1:T(8,128)(2,1)}) %all-gather.3.cloned.1.call-update) | async-done | bytes 3145744 | tf_op jit(solution)/shard_map/all_gather | solution.py:40
  137.7 3.3 %fusion.52 = (bf16[6144,128]{0,1:T(8,128)(2,1)S(1)}, bf16[6144,128]{0,1:T(8,128)(2,1)}) fusion(bf16[6144,256]{0,1:T(8,128)(2,1)} %all-gather.3.cloned.1.call-done), kind=kLoop, calls=%fused_computation.120 | loop fusion | bytes 6291456 | tf_op jit(solution)/shard_map/split | solution.py:41
  141.0 51.5 %while.40 = (s32[]{:T(128)}, f32[1,384]{1,0:T(1,128)S(1)}, f32[1,384]{1,0:T(1,128)S(1)}, f32[384,1,128]{0,2,1:T(8,128)S(1)}, s32[16]{0:T(128)S(1)}, /*index=5*/s...) while((s32[]{:T(128)}, f32[1,384]{1,0:T(1,128)S(1)}, ...), condition=%wide.region_15.16_spmd.clone, body=%wide.region_12.15_spmd.clone.sunk | while | flops 77416712 | bytes 2498263 | solution.py:196
  142.4 1.2 fusion.84
  145.7 1.2 fusion.84
  148.9 1.2 fusion.84
  174.6 1.2 fusion.84
  177.8 1.2 fusion.84
  181.1 1.2 fusion.84
  184.3 1.2 fusion.84
  193.1 33.0 %all_to_all.21 = bf16[32,12,1024]{2,1,0:T(8,128)(2,1)S(1)} all-to-all(bf16[32,12,1024]{2,1,0:T(8,128)(2,1)S(1)} %reshape.208), channel_id=1, replica_groups=mesh['bytes'=16,'ctx'=8,'tp'=4] {'ctx','tp'}, dimensions={0} | all-to-all | bytes 1572864 | tf_op jit(solution)/shard_map/all_to_all | solution.py:51
  227.4 4.8 %all-to-all-start.3 = ((bf16[32,12,1024]{2,1,0:T(8,128)(2,1)}), bf16[32,12,1024]{2,1,0:T(8,128)(2,1)S(1)}, u32[]{:S(2)}, u32[]{:S(2)}) async-start(bf16[32,12,1024]{2,1,0:T(8,128)(2,1)} %broadcast_in_dim.119), calls=%async_computation.3 | async-start | bytes 2097152 | tf_op jit(solution)/shard_map/all_to_all | solution.py:23
  233.6 14.9 %all-to-all-done.3 = bf16[32,12,1024]{2,1,0:T(8,128)(2,1)S(1)} async-done(((bf16[32,12,1024]{2,1,0:T(8,128)(2,1)}), bf16[32,12,1024]{2,1,0:T(8,128)(2,1)S(1)}, u32[]{:S(2)}, u32[]{:S(2)}) %all-to-all-start.3) | async-done | bytes 786464 | tf_op jit(solution)/shard_map/all_to_all | solution.py:23
  (300 shorter events, 55.1 us)
Async XLA Ops:
  6.5 15.8 %copy-start = (bf16[256,1024]{1,0:T(8,128)(2,1)S(1)}, bf16[256,1024]{1,0:T(8,128)(2,1)}, u32[]{:S(2)}) copy-start(bf16[256,1024]{1,0:T(8,128)(2,1)} %param.16) | copy-start | bytes 1572868
  6.5 24.7 %collective-permute-start = (s32[192]{0:T(256)}, s32[192]{0:T(256)S(1)}, u32[]{:S(2)}, u32[]{:S(2)}) collective-permute-start(s32[192]{0:T(256)} %param.14), channel_id=1, source_target_pairs={{0,4},{4,8},{8,12},{12,16},{16,20},{20,24},{24,28},{28,32},{32,36}... | collective-permute-start | bytes 2312 | tf_op jit(solution)/shard_map/ppermute | solution.py:18
  12.5 0.6 copy-start.13
  13.1 10.4 %copy-start.17 = (s32[192]{0:T(256)}, s32[192]{0:T(256)S(1)}, u32[]{:S(2)}) copy-start(s32[192]{0:T(256)S(1)} %slice_add_fusion) | copy-start | bytes 2308
  14.9 14.2 %all-to-all-start = ((s32[32,1,1]{2,1,0:T(1,128)}), s32[32,1,1]{2,1,0:T(1,128)S(1)}, u32[]{:S(2)}, u32[]{:S(2)}) async-start(s32[32,1,1]{2,1,0:T(1,128)} %broadcast_in_dim.111), calls=%async_computation | async-start | bytes 32768 | tf_op jit(solution)/shard_map/all_to_all | solution.py:23
  22.3 1.3 copy-start.1
  23.5 1.0 copy-start.4
  23.7 1.1 copy-start.2
  26.4 5.8 %copy-start.6 = (pred[192,384]{1,0:T(8,128)(4,1)}, pred[192,384]{1,0:T(8,128)(4,1)S(1)}, u32[]{:S(2)}) copy-start(pred[192,384]{1,0:T(8,128)(4,1)S(1)} %fusion.34) | copy-start | bytes 221188
  26.6 5.7 %copy-start.3 = (bf16[192,256]{0,1:T(8,128)(2,1)}, bf16[192,256]{0,1:T(8,128)(2,1)S(1)}, u32[]{:S(2)}) copy-start(bf16[192,256]{0,1:T(8,128)(2,1)S(1)} %copy.33) | copy-start | bytes 294916
  30.0 0.6 copy-start.15
  31.7 0.6 copy-start.11
  33.0 1.4 copy-start.12
  33.0 1.7 copy-start.5
  34.4 0.9 copy-start.7
  35.2 0.6 copy-start.18
  35.2 0.6 copy-start.22
  35.8 1.4 copy-start.9
  37.2 24.7 %all-to-all-start.1 = ((bf16[32,72,256]{2,1,0:T(8,128)(2,1)}), bf16[32,72,256]{2,1,0:T(8,128)(2,1)S(1)}, u32[]{:S(2)}, u32[]{:S(2)}) async-start(bf16[32,72,256]{2,1,0:T(8,128)(2,1)} %broadcast_in_dim.118), calls=%async_computation.1 | async-start | bytes 2359296 | tf_op jit(solution)/shard_map/all_to_all | solution.py:23
  42.0 95.8 %all-gather.3.cloned.1.call-start = ((), (), s32[]{:S(2)}) async-start(), calls=%async_computation.4 | async-start | bytes 3342336 | tf_op jit(solution)/shard_map/all_gather | solution.py:40
  62.7 2.3 copy-start.19
  64.7 1.0 copy-start.20
  66.9 32.2 %copy-start.21 = (bf16[1024,128]{1,0:T(8,128)(2,1)S(1)}, bf16[1024,128]{1,0:T(8,128)(2,1)}, u32[]{:S(2)}) copy-start(bf16[1024,128]{1,0:T(8,128)(2,1)} %param.20) | copy-start | bytes 786436
  141.0 51.5 %copy-start.8 = (bf16[128,1024]{1,0:T(8,128)(2,1)S(1)}, bf16[128,1024]{1,0:T(8,128)(2,1)}, u32[]{:S(2)}) copy-start(bf16[128,1024]{1,0:T(8,128)(2,1)} %param.23) | copy-start | bytes 786436
  227.4 4.8 %copy-start.16 = (s32[8]{0:T(128)S(1)}, s32[8]{0:T(128)}, u32[]{:S(2)}) copy-start(s32[8]{0:T(128)} %copy-done.15) | copy-start | bytes 100
  227.4 5.4 %copy-start.14 = (s32[256]{0:T(256)S(1)}, s32[256]{0:T(256)}, u32[]{:S(2)}) copy-start(s32[256]{0:T(256)} %copy-done.13) | copy-start | bytes 3076
  227.4 6.1 %copy-start.10 = (bf16[192,4,64]{0,2,1:T(8,128)(2,1)S(1)}, bf16[192,4,64]{0,2,1:T(8,128)(2,1)}, u32[]{:S(2)}) copy-start(bf16[192,4,64]{0,2,1:T(8,128)(2,1)} %copy-done.9) | copy-start | bytes 294916
  227.4 21.1 %all-to-all-start.3 = ((bf16[32,12,1024]{2,1,0:T(8,128)(2,1)}), bf16[32,12,1024]{2,1,0:T(8,128)(2,1)S(1)}, u32[]{:S(2)}, u32[]{:S(2)}) async-start(bf16[32,12,1024]{2,1,0:T(8,128)(2,1)} %broadcast_in_dim.119), calls=%async_computation.3 | async-start | bytes 2097152 | tf_op jit(solution)/shard_map/all_to_all | solution.py:23
Sparse Core Ops, SparseCore 0:
  67.0 70.6 all-gather.2
where the time goes:
time: 258 us; the launch traced here: 257 us
  blocking collectives  62 us (24%)
  waiting for transfers between devices  55.7 us (22%)
  local copies, waits for them, and re-layouts  47.7 us (18%)
  matrix products  32.5 us (13%)
  starting transfers between devices  21.5 us (8%)
  between operations  14.6 us (6%)
  loops' own time  12.5 us (5%)
  other arithmetic  10.6 us (4%)
    all_gather x1, waiting for transfers between devices, sent_together(): filled = lax.all_gather(both, axis, axis=dim, tiled=True)  38.2 us
    all_to_all x1, blocking collectives, sent_and_summed(): lax.all_to_all(tiles, axis, split_axis=0, concat_axis=0, tiled=True)  33 us
    all_gather x1, blocking collectives, per_device(): lax.all_gather(positions, 'bytes', axis=0, tiled=True)  29 us
    dot_general x16, matrix products, attend_block(): jnp.einsum('qhd,khd->hqk', queries_h, keys_s, preferred_element_type=jnp....  18.9 us
    gather x10, local copies, waits for them, and re-layouts, per_device(): jnp.searchsorted(running, targets + 1)  18.9 us
    all_to_all x3, waiting for transfers between devices, copy_for_each(): return lax.all_to_all(copies, axis, split_axis=0, concat_axis=0, tiled=True)  17.5 us
    all_to_all x3, starting transfers between devices, copy_for_each(): return lax.all_to_all(copies, axis, split_axis=0, concat_axis=0, tiled=True)  16.9 us
    another operation x1, loops' own time, per_device(): lax.scan(attend_block, running_state, jnp.arange(span_rows // query_rows,...  11.9 us
  transfers between devices with their start and end apart: 5, of which 3 were waited for; matrix products, arithmetic and copies ran while one was open for 12% of the time, Pallas kernels for 0%

commit v1 on v0

--- a/solution.py
+++ b/solution.py
@@ -10,6 +10,28 @@
 EPSILON = 1e-06
 NEGATIVE = -1e30
 FARAWAY = 1 << 30
+
+
+def joined_along_2(blocks, dim):
+    blocks = jnp.moveaxis(blocks, 0, dim)
+    shape = blocks.shape
+    return blocks.reshape(*shape[:dim], shape[dim] * shape[dim + 1], *shape[dim + 2 :])
+
+
+def collect_2(x, axis, dim):
+    length = lax.axis_size(axis)
+    pairs = [(i, (i + 1) % length) for i in range(length)]
+    back = [(b, a) for a, b in pairs]
+    lower, upper = ([], [])
+    for step in range(length - 1):
+        if step % 2 == 0:
+            lower.append(lax.ppermute(lower[-1] if lower else x, axis, pairs))
+        else:
+            upper.append(lax.ppermute(upper[-1] if upper else x, axis, back))
+    tiles = jnp.stack([*lower[::-1], x, *upper])
+    shift = lax.axis_index(axis) - len(lower)
+    tiles = tiles[(jnp.arange(length) - shift) % length]
+    return joined_along_2(tiles, dim)
 
 
 def from_behind(value, axis, steps):
@@ -161,7 +183,7 @@
     running_state = initial
     keys_p, values_p, places_p = (
         *sent_together((keys_l, values_l), "bytes", 0, 1),
-        lax.all_gather(positions, "bytes", axis=0, tiled=True),
+        collect_2(positions, "bytes", 0),
     )
     span_rows = keys_p.shape[0]
 

time: 258 us -> 255 us (0.988)
  starting transfers between devices: 21.5 us -> 74.4 us
  blocking collectives: 62 us -> 32.9 us
  waiting for transfers between devices: 55.7 us -> 30.7 us
    ppermute x0 -> x15, starting transfers between devices: none -> 53.6 us  [the longest x7 36.6 us: collect_2(): upper.append(lax.ppermute(upper[-1] if upper else x, axis, back))]
    all_gather x1, waiting for transfers between devices: 38.2 us -> 9.2 us  [sent_together(): filled = lax.all_gather(both, axis, axis=dim, tiled=True)]
    all_gather x1 -> x0, blocking collectives: 29 us -> none  [per_device(): lax.all_gather(positions, 'bytes', axis=0, tiled=True)]
    ppermute x0 -> x15, waiting for transfers between devices: none -> 2.84 us  [the longest x8 2.82 us: collect_2(): lower.append(lax.ppermute(lower[-1] if lower else x, axis, pairs))]
  transfers between devices with their start and end apart: 5 -> 20, of which waited for: 3 -> 4; matrix products, arithmetic and copies ran while one was open for 12% -> 13% of each run, Pallas kernels for 0% -> 0%
where the time goes in v1:
time: 255 us; the launch traced here: 254 us
  starting transfers between devices  74.4 us (29%)
  local copies, waits for them, and re-layouts  46.9 us (18%)
  blocking collectives  32.9 us (13%)
  matrix products  31 us (12%)
  waiting for transfers between devices  30.7 us (12%)
  between operations  14.9 us (6%)
  loops' own time  12.4 us (5%)
  other arithmetic  10.7 us (4%)
    ppermute x7, starting transfers between devices, collect_2(): upper.append(lax.ppermute(upper[-1] if upper else x, axis, back))  36.6 us
    all_to_all x1, blocking collectives, sent_and_summed(): lax.all_to_all(tiles, axis, split_axis=0, concat_axis=0, tiled=True)  32.9 us
    dot_general x16, matrix products, attend_block(): jnp.einsum('qhd,khd->hqk', queries_h, keys_s, preferred_element_type=jnp....  19 us
    gather x10, local copies, waits for them, and re-layouts, per_device(): jnp.searchsorted(running, targets + 1)  18.9 us
    all_to_all x3, waiting for transfers between devices, copy_for_each(): return lax.all_to_all(copies, axis, split_axis=0, concat_axis=0, tiled=True)  18.6 us
    ppermute x8, starting transfers between devices, collect_2(): lower.append(lax.ppermute(lower[-1] if lower else x, axis, pairs))  17 us
    all_to_all x3, starting transfers between devices, copy_for_each(): return lax.all_to_all(copies, axis, split_axis=0, concat_axis=0, tiled=True)  16.2 us
    another operation x1, loops' own time, per_device(): lax.scan(attend_block, running_state, jnp.arange(span_rows // query_rows,...  11.9 us
  transfers between devices with their start and end apart: 20, of which 4 were waited for; matrix products, arithmetic and copies ran while one was open for 13% of the time, Pallas kernels for 0%

profile of v1, /device:TPU:1, one launch (start us, length us, event | category | flops | bytes accessed | tf_op | source)
XLA Modules:
  0.0 253.9 jit_solution(942530859513558394)
XLA Ops:
  6.5 4.6 %collective-permute-start = (s32[192]{0:T(256)}, s32[192]{0:T(256)S(1)}, u32[]{:S(2)}, u32[]{:S(2)}) collective-permute-start(s32[192]{0:T(256)} %param.14), channel_id=1, source_target_pairs={{0,4},{4,8},{8,12},{12,16},{16,20},{20,24},{24,28},{28,32},{32,36}... | collective-permute-start | bytes 2312 | tf_op jit(solution)/shard_map/ppermute | solution.py:40
  14.3 7.3 %all-to-all-start = ((s32[32,1,1]{2,1,0:T(1,128)}), s32[32,1,1]{2,1,0:T(1,128)S(1)}, u32[]{:S(2)}, u32[]{:S(2)}) async-start(s32[32,1,1]{2,1,0:T(1,128)} %broadcast_in_dim.114), calls=%async_computation | async-start | bytes 32768 | tf_op jit(solution)/shard_map/all_to_all | solution.py:45
  24.8 3.7 %all-to-all-done = s32[32,1,1]{2,1,0:T(1,128)S(1)} async-done(((s32[32,1,1]{2,1,0:T(1,128)}), s32[32,1,1]{2,1,0:T(1,128)S(1)}, u32[]{:S(2)}, u32[]{:S(2)}) %all-to-all-start) | async-done | bytes 160 | tf_op jit(solution)/shard_map/all_to_all | solution.py:45
  34.5 4.3 %all-to-all-start.1 = ((bf16[32,72,256]{2,1,0:T(8,128)(2,1)}), bf16[32,72,256]{2,1,0:T(8,128)(2,1)S(1)}, u32[]{:S(2)}, u32[]{:S(2)}) async-start(bf16[32,72,256]{2,1,0:T(8,128)(2,1)} %broadcast_in_dim.122), calls=%async_computation.1 | async-start | bytes 2359296 | tf_op jit(solution)/shard_map/all_to_all | solution.py:45
  38.8 19.8 %while.39 = (s32[]{:T(128)}, u32[384]{0:T(512)S(1)}, u32[384]{0:T(512)S(1)}, s32[576]{0:T(1024)S(1)}, s32[]{:T(128)}, /*index=5*/s32[]{:T(128)}, s32[]{}) while((s32[]{:T(128)}, u32[384]{0:T(512)S(1)}, u32[384]{0:T(512)S(1)}, s32[576]{0:T(1024)S(1)}, s32[]{:T(128)}, /*index=5*/s32[]{:T(128)}, s32[]{}) %tuple.72), condition=%wide.region_10.11_spmd.clone, body=%wide.region_9.10_spmd.clone.sunk | while | flops 8324 | bytes 29541 | solution.py:168
  38.9 1.9 gather_fusion
  42.8 1.9 gather_fusion
  44.8 1.9 gather_fusion
  50.8 1.9 gather_fusion
  59.5 2.1 gather_fusion.3
  66.9 3.5 %collective-permute-start.1 = (s32[384]{0:T(512)S(1)}, s32[384]{0:T(512)S(1)}, u32[]{:S(2)}, u32[]{:S(2)}) collective-permute-start(s32[384]{0:T(512)S(1)} %fusion.42), channel_id=1, source_target_pairs={{0,32},{32,64},{64,96},{96,128},{128,160},{160,192},{192,224},{224... | collective-permute-start | bytes 4616 | tf_op jit(solution)/shard_map/ppermute | solution.py:28
  70.4 9.1 %collective-permute-start.9 = (s32[384]{0:T(512)S(1)}, s32[384]{0:T(512)S(1)}, u32[]{:S(2)}, u32[]{:S(2)}) collective-permute-start(s32[384]{0:T(512)S(1)} %fusion.42), channel_id=1, source_target_pairs={{32,0},{64,32},{96,64},{128,96},{160,128},{192,160},{224,192},{256... | collective-permute-start | bytes 4616 | tf_op jit(solution)/shard_map/ppermute | solution.py:30
  79.6 1.9 collective-permute-start.2
  81.5 4.6 %collective-permute-start.10 = (s32[384]{0:T(512)S(1)}, s32[384]{0:T(512)S(1)}, u32[]{:S(2)}, u32[]{:S(2)}) collective-permute-start(s32[384]{0:T(512)S(1)} %collective-permute-done.9), channel_id=1, source_target_pairs={{32,0},{64,32},{96,64},{128,96},{160,128},{192,160},{224,192},{256... | collective-permute-start | bytes 4616 | tf_op jit(solution)/shard_map/ppermute | solution.py:30
  86.1 1.9 collective-permute-start.3
  88.0 4.6 %collective-permute-start.11 = (s32[384]{0:T(512)S(1)}, s32[384]{0:T(512)S(1)}, u32[]{:S(2)}, u32[]{:S(2)}) collective-permute-start(s32[384]{0:T(512)S(1)} %collective-permute-done.10), channel_id=1, source_target_pairs={{32,0},{64,32},{96,64},{128,96},{160,128},{192,160},{224,192},{256... | collective-permute-start | bytes 4616 | tf_op jit(solution)/shard_map/ppermute | solution.py:30
  92.6 1.9 collective-permute-start.4
  94.6 4.6 %collective-permute-start.12 = (s32[384]{0:T(512)S(1)}, s32[384]{0:T(512)S(1)}, u32[]{:S(2)}, u32[]{:S(2)}) collective-permute-start(s32[384]{0:T(512)S(1)} %collective-permute-done.11), channel_id=1, source_target_pairs={{32,0},{64,32},{96,64},{128,96},{160,128},{192,160},{224,192},{256... | collective-permute-start | bytes 4616 | tf_op jit(solution)/shard_map/ppermute | solution.py:30
  99.2 1.9 collective-permute-start.5
  101.1 4.6 %collective-permute-start.13 = (s32[384]{0:T(512)S(1)}, s32[384]{0:T(512)S(1)}, u32[]{:S(2)}, u32[]{:S(2)}) collective-permute-start(s32[384]{0:T(512)S(1)} %collective-permute-done.12), channel_id=1, source_target_pairs={{32,0},{64,32},{96,64},{128,96},{160,128},{192,160},{224,192},{256... | collective-permute-start | bytes 4616 | tf_op jit(solution)/shard_map/ppermute | solution.py:30
  105.7 1.9 collective-permute-start.6
  107.7 4.6 %collective-permute-start.14 = (s32[384]{0:T(512)S(1)}, s32[384]{0:T(512)S(1)}, u32[]{:S(2)}, u32[]{:S(2)}) collective-permute-start(s32[384]{0:T(512)S(1)} %collective-permute-done.13), channel_id=1, source_target_pairs={{32,0},{64,32},{96,64},{128,96},{160,128},{192,160},{224,192},{256... | collective-permute-start | bytes 4616 | tf_op jit(solution)/shard_map/ppermute | solution.py:30
  112.2 1.9 collective-permute-start.7
  114.2 4.6 %collective-permute-start.15 = (s32[384]{0:T(512)S(1)}, s32[384]{0:T(512)S(1)}, u32[]{:S(2)}, u32[]{:S(2)}) collective-permute-start(s32[384]{0:T(512)S(1)} %collective-permute-done.14), channel_id=1, source_target_pairs={{32,0},{64,32},{96,64},{128,96},{160,128},{192,160},{224,192},{256... | collective-permute-start | bytes 4616 | tf_op jit(solution)/shard_map/ppermute | solution.py:30
  118.8 1.9 collective-permute-start.8
  121.6 2.8 %collective-permute-done.8 = s32[384]{0:T(512)S(1)} collective-permute-done((s32[384]{0:T(512)S(1)}, s32[384]{0:T(512)S(1)}, u32[]{:S(2)}, u32[]{:S(2)}) %collective-permute-start.8) | collective-permute-done | bytes 1568 | tf_op jit(solution)/shard_map/ppermute | solution.py:28
  125.4 9.2 %all-gather.2.cloned.1.call-done = bf16[6144,256]{0,1:T(8,128)(2,1)} async-done(((bf16[384,256]{0,1:T(8,128)(2,1)}), bf16[6144,256]{0,1:T(8,128)(2,1)}) %all-gather.2.cloned.1.call-update) | async-done | bytes 3145744 | tf_op jit(solution)/shard_map/all_gather | solution.py:62
  134.7 3.3 %fusion.54 = (bf16[6144,128]{0,1:T(8,128)(2,1)S(1)}, bf16[6144,128]{0,1:T(8,128)(2,1)}) fusion(bf16[6144,256]{0,1:T(8,128)(2,1)} %all-gather.2.cloned.1.call-done), kind=kLoop, calls=%fused_computation.129 | loop fusion | bytes 6291456 | tf_op jit(solution)/shard_map/split | solution.py:63
  137.9 51.5 %while.40 = (s32[]{:T(128)}, f32[1,384]{1,0:T(1,128)S(1)}, f32[1,384]{1,0:T(1,128)S(1)}, f32[384,1,128]{0,2,1:T(8,128)S(1)}, s32[16]{0:T(128)S(1)}, /*index=5*/s...) while((s32[]{:T(128)}, f32[1,384]{1,0:T(1,128)S(1)}, ...), condition=%wide.region_15.16_spmd.clone, body=%wide.region_12.15_spmd.clone.sunk | while | flops 77416712 | bytes 2498271 | solution.py:218
  190.1 32.9 %all_to_all.21 = bf16[32,12,1024]{2,1,0:T(8,128)(2,1)S(1)} all-to-all(bf16[32,12,1024]{2,1,0:T(8,128)(2,1)S(1)} %reshape.275), channel_id=1, replica_groups=mesh['bytes'=16,'ctx'=8,'tp'=4] {'ctx','tp'}, dimensions={0} | all-to-all | bytes 1572864 | tf_op jit(solution)/shard_map/all_to_all | solution.py:73
  224.3 4.6 %all-to-all-start.3 = ((bf16[32,12,1024]{2,1,0:T(8,128)(2,1)}), bf16[32,12,1024]{2,1,0:T(8,128)(2,1)S(1)}, u32[]{:S(2)}, u32[]{:S(2)}) async-start(bf16[32,12,1024]{2,1,0:T(8,128)(2,1)} %broadcast_in_dim.123), calls=%async_computation.3 | async-start | bytes 2097152 | tf_op jit(solution)/shard_map/all_to_all | solution.py:45
  230.4 14.9 %all-to-all-done.3 = bf16[32,12,1024]{2,1,0:T(8,128)(2,1)S(1)} async-done(((bf16[32,12,1024]{2,1,0:T(8,128)(2,1)}), bf16[32,12,1024]{2,1,0:T(8,128)(2,1)S(1)}, u32[]{:S(2)}, u32[]{:S(2)}) %all-to-all-start.3) | async-done | bytes 786464 | tf_op jit(solution)/shard_map/all_to_all | solution.py:45
  (319 shorter events, 75.8 us)
Async XLA Ops:
  6.5 15.3 %copy-start = (bf16[256,1024]{1,0:T(8,128)(2,1)S(1)}, bf16[256,1024]{1,0:T(8,128)(2,1)}, u32[]{:S(2)}) copy-start(bf16[256,1024]{1,0:T(8,128)(2,1)} %param.16) | copy-start | bytes 1572868
  6.5 23.6 %collective-permute-start = (s32[192]{0:T(256)}, s32[192]{0:T(256)S(1)}, u32[]{:S(2)}, u32[]{:S(2)}) collective-permute-start(s32[192]{0:T(256)} %param.14), channel_id=1, source_target_pairs={{0,4},{4,8},{8,12},{12,16},{16,20},{20,24},{24,28},{28,32},{32,36}... | collective-permute-start | bytes 2312 | tf_op jit(solution)/shard_map/ppermute | solution.py:40
  14.3 14.2 %all-to-all-start = ((s32[32,1,1]{2,1,0:T(1,128)}), s32[32,1,1]{2,1,0:T(1,128)S(1)}, u32[]{:S(2)}, u32[]{:S(2)}) async-start(s32[32,1,1]{2,1,0:T(1,128)} %broadcast_in_dim.114), calls=%async_computation | async-start | bytes 32768 | tf_op jit(solution)/shard_map/all_to_all | solution.py:45
  21.8 1.3 copy-start.1
  23.0 1.0 copy-start.3
  23.1 1.2 copy-start.2
  34.5 24.2 %all-to-all-start.1 = ((bf16[32,72,256]{2,1,0:T(8,128)(2,1)}), bf16[32,72,256]{2,1,0:T(8,128)(2,1)S(1)}, u32[]{:S(2)}, u32[]{:S(2)}) async-start(bf16[32,72,256]{2,1,0:T(8,128)(2,1)} %broadcast_in_dim.122), calls=%async_computation.1 | async-start | bytes 2359296 | tf_op jit(solution)/shard_map/all_to_all | solution.py:45
  38.8 95.9 %all-gather.2.cloned.1.call-start = ((), (), s32[]{:S(2)}) async-start(), calls=%async_computation.4 | async-start | bytes 3342336 | tf_op jit(solution)/shard_map/all_gather | solution.py:62
  59.4 2.3 copy-start.5
  61.5 1.0 copy-start.6
  64.3 60.7 %copy-start.7 = (bf16[1024,128]{1,0:T(8,128)(2,1)S(1)}, bf16[1024,128]{1,0:T(8,128)(2,1)}, u32[]{:S(2)}) copy-start(bf16[1024,128]{1,0:T(8,128)(2,1)} %param.20) | copy-start | bytes 786436
  66.9 12.7 %collective-permute-start.1 = (s32[384]{0:T(512)S(1)}, s32[384]{0:T(512)S(1)}, u32[]{:S(2)}, u32[]{:S(2)}) collective-permute-start(s32[384]{0:T(512)S(1)} %fusion.42), channel_id=1, source_target_pairs={{0,32},{32,64},{64,96},{96,128},{128,160},{160,192},{192,224},{224... | collective-permute-start | bytes 4616 | tf_op jit(solution)/shard_map/ppermute | solution.py:28
  70.4 11.1 %collective-permute-start.9 = (s32[384]{0:T(512)S(1)}, s32[384]{0:T(512)S(1)}, u32[]{:S(2)}, u32[]{:S(2)}) collective-permute-start(s32[384]{0:T(512)S(1)} %fusion.42), channel_id=1, source_target_pairs={{32,0},{64,32},{96,64},{128,96},{160,128},{192,160},{224,192},{256... | collective-permute-start | bytes 4616 | tf_op jit(solution)/shard_map/ppermute | solution.py:30
  79.6 6.5 %collective-permute-start.2 = (s32[384]{0:T(512)S(1)}, s32[384]{0:T(512)S(1)}, u32[]{:S(2)}, u32[]{:S(2)}) collective-permute-start(s32[384]{0:T(512)S(1)} %collective-permute-done.1), channel_id=1, source_target_pairs={{0,32},{32,64},{64,96},{96,128},{128,160},{160,192},{192,224},{224... | collective-permute-start | bytes 4616 | tf_op jit(solution)/shard_map/ppermute | solution.py:28
  81.5 6.5 %collective-permute-start.10 = (s32[384]{0:T(512)S(1)}, s32[384]{0:T(512)S(1)}, u32[]{:S(2)}, u32[]{:S(2)}) collective-permute-start(s32[384]{0:T(512)S(1)} %collective-permute-done.9), channel_id=1, source_target_pairs={{32,0},{64,32},{96,64},{128,96},{160,128},{192,160},{224,192},{256... | collective-permute-start | bytes 4616 | tf_op jit(solution)/shard_map/ppermute | solution.py:30
  86.1 6.5 %collective-permute-start.3 = (s32[384]{0:T(512)S(1)}, s32[384]{0:T(512)S(1)}, u32[]{:S(2)}, u32[]{:S(2)}) collective-permute-start(s32[384]{0:T(512)S(1)} %collective-permute-done.2), channel_id=1, source_target_pairs={{0,32},{32,64},{64,96},{96,128},{128,160},{160,192},{192,224},{224... | collective-permute-start | bytes 4616 | tf_op jit(solution)/shard_map/ppermute | solution.py:28
  88.0 6.5 %collective-permute-start.11 = (s32[384]{0:T(512)S(1)}, s32[384]{0:T(512)S(1)}, u32[]{:S(2)}, u32[]{:S(2)}) collective-permute-start(s32[384]{0:T(512)S(1)} %collective-permute-done.10), channel_id=1, source_target_pairs={{32,0},{64,32},{96,64},{128,96},{160,128},{192,160},{224,192},{256... | collective-permute-start | bytes 4616 | tf_op jit(solution)/shard_map/ppermute | solution.py:30
  92.6 6.5 %collective-permute-start.4 = (s32[384]{0:T(512)S(1)}, s32[384]{0:T(512)S(1)}, u32[]{:S(2)}, u32[]{:S(2)}) collective-permute-start(s32[384]{0:T(512)S(1)} %collective-permute-done.3), channel_id=1, source_target_pairs={{0,32},{32,64},{64,96},{96,128},{128,160},{160,192},{192,224},{224... | collective-permute-start | bytes 4616 | tf_op jit(solution)/shard_map/ppermute | solution.py:28
  94.6 6.5 %collective-permute-start.12 = (s32[384]{0:T(512)S(1)}, s32[384]{0:T(512)S(1)}, u32[]{:S(2)}, u32[]{:S(2)}) collective-permute-start(s32[384]{0:T(512)S(1)} %collective-permute-done.11), channel_id=1, source_target_pairs={{32,0},{64,32},{96,64},{128,96},{160,128},{192,160},{224,192},{256... | collective-permute-start | bytes 4616 | tf_op jit(solution)/shard_map/ppermute | solution.py:30
  99.2 6.5 %collective-permute-start.5 = (s32[384]{0:T(512)S(1)}, s32[384]{0:T(512)S(1)}, u32[]{:S(2)}, u32[]{:S(2)}) collective-permute-start(s32[384]{0:T(512)S(1)} %collective-permute-done.4), channel_id=1, source_target_pairs={{0,32},{32,64},{64,96},{96,128},{128,160},{160,192},{192,224},{224... | collective-permute-start | bytes 4616 | tf_op jit(solution)/shard_map/ppermute | solution.py:28
  101.1 6.5 %collective-permute-start.13 = (s32[384]{0:T(512)S(1)}, s32[384]{0:T(512)S(1)}, u32[]{:S(2)}, u32[]{:S(2)}) collective-permute-start(s32[384]{0:T(512)S(1)} %collective-permute-done.12), channel_id=1, source_target_pairs={{32,0},{64,32},{96,64},{128,96},{160,128},{192,160},{224,192},{256... | collective-permute-start | bytes 4616 | tf_op jit(solution)/shard_map/ppermute | solution.py:30
  105.7 6.5 %collective-permute-start.6 = (s32[384]{0:T(512)S(1)}, s32[384]{0:T(512)S(1)}, u32[]{:S(2)}, u32[]{:S(2)}) collective-permute-start(s32[384]{0:T(512)S(1)} %collective-permute-done.5), channel_id=1, source_target_pairs={{0,32},{32,64},{64,96},{96,128},{128,160},{160,192},{192,224},{224... | collective-permute-start | bytes 4616 | tf_op jit(solution)/shard_map/ppermute | solution.py:28
  107.7 6.6 %collective-permute-start.14 = (s32[384]{0:T(512)S(1)}, s32[384]{0:T(512)S(1)}, u32[]{:S(2)}, u32[]{:S(2)}) collective-permute-start(s32[384]{0:T(512)S(1)} %collective-permute-done.13), channel_id=1, source_target_pairs={{32,0},{64,32},{96,64},{128,96},{160,128},{192,160},{224,192},{256... | collective-permute-start | bytes 4616 | tf_op jit(solution)/shard_map/ppermute | solution.py:30
  112.2 6.6 %collective-permute-start.7 = (s32[384]{0:T(512)S(1)}, s32[384]{0:T(512)S(1)}, u32[]{:S(2)}, u32[]{:S(2)}) collective-permute-start(s32[384]{0:T(512)S(1)} %collective-permute-done.6), channel_id=1, source_target_pairs={{0,32},{32,64},{64,96},{96,128},{128,160},{160,192},{192,224},{224... | collective-permute-start | bytes 4616 | tf_op jit(solution)/shard_map/ppermute | solution.py:28
  114.2 7.3 %collective-permute-start.15 = (s32[384]{0:T(512)S(1)}, s32[384]{0:T(512)S(1)}, u32[]{:S(2)}, u32[]{:S(2)}) collective-permute-start(s32[384]{0:T(512)S(1)} %collective-permute-done.14), channel_id=1, source_target_pairs={{32,0},{64,32},{96,64},{128,96},{160,128},{192,160},{224,192},{256... | collective-permute-start | bytes 4616 | tf_op jit(solution)/shard_map/ppermute | solution.py:30
  118.8 5.5 %collective-permute-start.8 = (s32[384]{0:T(512)S(1)}, s32[384]{0:T(512)S(1)}, u32[]{:S(2)}, u32[]{:S(2)}) collective-permute-start(s32[384]{0:T(512)S(1)} %collective-permute-done.7), channel_id=1, source_target_pairs={{0,32},{32,64},{64,96},{96,128},{128,160},{160,192},{192,224},{224... | collective-permute-start | bytes 4616 | tf_op jit(solution)/shard_map/ppermute | solution.py:28
  137.9 51.6 %copy-start.4 = (bf16[128,1024]{1,0:T(8,128)(2,1)S(1)}, bf16[128,1024]{1,0:T(8,128)(2,1)}, u32[]{:S(2)}) copy-start(bf16[128,1024]{1,0:T(8,128)(2,1)} %param.23) | copy-start | bytes 786436
  224.3 21.0 %all-to-all-start.3 = ((bf16[32,12,1024]{2,1,0:T(8,128)(2,1)}), bf16[32,12,1024]{2,1,0:T(8,128)(2,1)S(1)}, u32[]{:S(2)}, u32[]{:S(2)}) async-start(bf16[32,12,1024]{2,1,0:T(8,128)(2,1)} %broadcast_in_dim.123), calls=%async_computation.3 | async-start | bytes 2097152 | tf_op jit(solution)/shard_map/all_to_all | solution.py:45
Sparse Core Ops, SparseCore 0:
  63.8 70.7 all-gather.1
